TPU v7x, 256 devices: a whole 4x4x8 slice. The times are simulated.
256 devices in a mesh: ep: 16 (over z, core), fsdp: 4 (over x), tp: 4 (over y).
Axes of the slice: x: 4, y: 4, z: 8, core: 2. Of those that a mesh axis runs over, the one named last changes fastest.
Arguments:
- out_grad: bfloat16 [8192, 4096], P(('ep', 'fsdp')), may hold values from -1.5 to 1.5
- routes: int32 [8192, 2], P(('ep', 'fsdp')), may hold values from 0 to 15, all different within a row; in each aligned block of 128 rows (0 to 127, 128 to 255, ...) at most 32 rows name the same one
- chosen_logits: float32 [8192, 2], P(('ep', 'fsdp')), may hold values from -4 to 4
- routed_inputs: bfloat16 [16, 16, 4, 32, 4096], P('ep', None, 'fsdp'), may hold values from -6 to 6
- w_gate: bfloat16 [16, 4096, 1024], P('ep', 'fsdp', 'tp'), may hold values from -0.09375 to 0.09375
- w_up: bfloat16 [16, 4096, 1024], P('ep', 'fsdp', 'tp'), may hold values from -0.09375 to 0.09375
- w_down: bfloat16 [16, 1024, 4096], P('ep', 'tp', 'fsdp'), may hold values from -0.1875 to 0.1875
Outputs:
- input_grad: bfloat16 [8192, 4096], P(('ep', 'fsdp'))
- logit_grad: float32 [8192, 2], P(('ep', 'fsdp'))
- grad_gate: float32 [16, 4096, 1024], P('ep', 'fsdp', 'tp')
- grad_up: float32 [16, 4096, 1024], P('ep', 'fsdp', 'tp')
- grad_down: float32 [16, 1024, 4096], P('ep', 'tp', 'fsdp')
Inputs may be any that keep to these rules, and one draw needn't show every extreme that they name: Each row of routes names 2 different experts. In each token group of 128 consecutive rows no expert is named by more than 32 rows, a bound that some block reaches.
All inputs are finite; a program needn't handle non-finite values.
Results may differ from a plain program's by a relative error of at most 0.015.
Values may be sent and summed in bfloat16 or wider, within the bound.
A program may use at most 128 MiB of HBM per device.

v0:
```python
import jax
import jax.numpy as jnp
from jax import lax
from jax.sharding import PartitionSpec as P


def laid_out(parts, dim):
    shape = list(parts.shape[1:])
    shape[dim] *= parts.shape[0]
    return jnp.moveaxis(parts, 0, dim).reshape(shape)


def gather_together(arrays, axis, dims):
    ravelled = jnp.concatenate([a.reshape(-1) for a in arrays])
    lines, at, outs = (lax.all_gather(ravelled, axis), 0, [])
    for a, dim in zip(arrays, dims):
        parts = lines[:, at : at + a.size].reshape(-1, *a.shape)
        outs.append(laid_out(parts, dim))
        at += a.size
    return tuple(outs)


def own_rows(product, width, axis):
    whole = product(jnp.int32(0), width * lax.axis_size(axis)).astype(jnp.bfloat16)
    return lax.psum_scatter(whole, axis, scatter_dimension=0, tiled=True).astype(jnp.float32)


def slot_places(routes, experts, capacity):
    flat_routes = routes.reshape(-1)
    onehot = (flat_routes[:, None] == jnp.arange(experts, dtype=jnp.int32)[None, :]).astype(
        jnp.int32
    )
    earlier = (jnp.cumsum(onehot, axis=0) - onehot).astype(jnp.int32)
    position = jnp.sum(earlier * onehot, axis=1).astype(jnp.int32)
    return (flat_routes * capacity + position).astype(jnp.int32)


def weighted_rows(grad_rows, gate_probs):
    scaled = gate_probs[:, :, None] * grad_rows.astype(jnp.float32)[:, None, :]
    return scaled.astype(jnp.bfloat16).reshape(-1, grad_rows.shape[1])


def fill_slots(values, slot_index, total_slots):
    row_total = values.shape[0]
    source = jnp.full((total_slots,), row_total, jnp.int32)
    source = source.at[slot_index].set(jnp.arange(row_total, dtype=jnp.int32))
    padded = jnp.concatenate([values, jnp.zeros((1, values.shape[1]), values.dtype)], axis=0)
    return jnp.take(padded, source, axis=0)


def combine(returned, slot_index, tokens, per_token):
    picked = jnp.take(returned, slot_index, axis=0).astype(jnp.float32)
    return jnp.sum(picked.reshape(tokens, per_token, -1), axis=1).astype(jnp.bfloat16)


def transpose_dot(left, right):
    return lax.dot_general(
        left, right, (((0,), (0,)), ((), ())), preferred_element_type=jnp.float32
    )


def contract_last(left, right):
    return lax.dot_general(
        left, right, (((1,), (1,)), ((), ())), preferred_element_type=jnp.float32
    )


def on_device(out_grad, routes, chosen_logits, routed_inputs, w_gate, w_up, w_down):
    experts = lax.axis_size("ep")
    tp_count = lax.axis_size("tp")
    tokens, model_width = out_grad.shape
    per_token = routes.shape[1]
    capacity = routed_inputs.shape[3]
    gate_probs = jax.nn.softmax(chosen_logits, axis=-1)
    slot_index = slot_places(routes, experts, capacity)
    inputs = routed_inputs.reshape(-1, model_width)
    narrow = model_width // tp_count
    column_piece = lax.dynamic_slice_in_dim(out_grad, lax.axis_index("tp") * narrow, narrow, 1)
    outgoing = fill_slots(weighted_rows(column_piece, gate_probs), slot_index, experts * capacity)
    arrived = lax.all_to_all(
        outgoing.reshape(experts, capacity, narrow), "ep", split_axis=0, concat_axis=0, tiled=True
    )
    scaled = lax.all_gather(arrived.reshape(-1, narrow), "tp", axis=1, tiled=True)
    gate_full, up_full, down_full = gather_together((w_gate, w_up, w_down), "fsdp", (1, 1, 2))
    gate_full = gate_full[0]
    up_full = up_full[0]
    down_full = down_full[0]
    gate_act = jnp.dot(inputs, gate_full, preferred_element_type=jnp.float32)
    up_act = jnp.dot(inputs, up_full, preferred_element_type=jnp.float32)
    sigmoid_gate = jax.nn.sigmoid(gate_act)
    silu_gate = gate_act * sigmoid_gate
    hidden = (silu_gate * up_act).astype(jnp.bfloat16)
    hidden_grad = contract_last(scaled, down_full)
    products = jnp.sum(hidden_grad * hidden.astype(jnp.float32), axis=1)
    up_grad = (hidden_grad * silu_gate).astype(jnp.bfloat16)
    gate_grad = (
        hidden_grad * up_act * sigmoid_gate * (1.0 + gate_act * (1.0 - sigmoid_gate))
    ).astype(jnp.bfloat16)
    slot_part = contract_last(gate_grad, gate_full) + contract_last(up_grad, up_full)
    pair_grads = jnp.concatenate([gate_grad, up_grad], axis=1)

    def grad_term(first_row, row_count):
        input_cols = lax.dynamic_slice_in_dim(inputs, first_row, row_count, 1)
        scaled_cols = lax.dynamic_slice_in_dim(scaled, first_row, row_count, 1)
        gate_up_part = transpose_dot(input_cols, pair_grads)
        down_part = transpose_dot(scaled_cols, hidden)
        return jnp.concatenate([gate_up_part, down_part], axis=1)

    grad_rows = own_rows(grad_term, model_width // lax.axis_size("fsdp"), "fsdp")
    hidden_units = hidden.shape[1]
    grad_gate = grad_rows[:, :hidden_units][None]
    grad_up = grad_rows[:, hidden_units : 2 * hidden_units][None]
    grad_down = grad_rows[:, 2 * hidden_units :].T[None]
    narrow = model_width // tp_count
    column_sum = lax.psum_scatter(
        slot_part.astype(jnp.bfloat16), "tp", scatter_dimension=1, tiled=True
    ).astype(jnp.float32)
    product_sum = lax.psum(products.astype(jnp.bfloat16), "tp").astype(jnp.float32)
    leaving = (
        column_sum.astype(jnp.bfloat16).reshape(experts, capacity, narrow),
        product_sum.astype(jnp.bfloat16).reshape(experts, capacity),
    )
    back_rows, back_products = (
        lax.all_to_all(leaving[0], "ep", split_axis=0, concat_axis=0, tiled=True),
        lax.all_to_all(leaving[1], "ep", split_axis=0, concat_axis=0, tiled=True),
    )
    combined = combine(back_rows.reshape(-1, narrow), slot_index, tokens, per_token)
    input_grad = lax.all_gather(combined, "tp", axis=1, tiled=True)
    chosen = (
        jnp.take(back_products.reshape(-1), slot_index)
        .astype(jnp.float32)
        .reshape(tokens, per_token)
    )
    logit_grad = chosen - gate_probs * jnp.sum(chosen, axis=1, keepdims=True)
    return (input_grad, logit_grad, grad_gate, grad_up, grad_down)


def solution(mesh):
    return jax.shard_map(
        on_device,
        mesh=mesh,
        in_specs=(
            P(("ep", "fsdp"), None),
            P(("ep", "fsdp"), None),
            P(("ep", "fsdp"), None),
            P("ep", None, "fsdp", None, None),
            P("ep", "fsdp", "tp"),
            P("ep", "fsdp", "tp"),
            P("ep", "tp", "fsdp"),
        ),
        out_specs=(
            P(("ep", "fsdp"), None),
            P(("ep", "fsdp"), None),
            P("ep", "fsdp", "tp"),
            P("ep", "fsdp", "tp"),
            P("ep", "tp", "fsdp"),
        ),
        check_vma=False,
    )
```

profile of v0, /device:TPU:1, one launch (start us, length us, event | category | flops | bytes accessed | tf_op | source)
XLA Modules:
  0.0 340.7 jit_solution(7325050296816589945)
XLA Ops:
  7.2 1.5 copy.58
  8.7 1.5 copy.59
  10.1 1.1 copy.60
  11.3 1.2 pad_maximum_fusion.1
  12.6 0.1 copy.45
  12.7 0.1 eq.26
  12.9 0.1 reshape.128
  13.0 1.0 dynamic-slice_convert_fusion
  14.0 0.4 mul.83
  14.4 0.7 mul.84
  15.2 0.1 copy.51
  15.3 0.1 mul.80
  15.5 0.6 reduce-window.6
  16.1 0.2 slice_reduce_fusion
  16.3 0.1 copy.50
  16.4 0.1 mul.79
  16.6 0.1 fusion.8
  16.7 1.4 scatter_custom_fusion
  18.1 0.1 broadcast_in_dim.52
  18.2 0.1 multiply_convert_fusion
  18.4 2.1 gather_fusion
  20.4 0.2 broadcast_select_fusion
  20.6 38.3 %all_to_all.19 = bf16[16,32,1024]{2,1,0:T(8,128)(2,1)} all-to-all(bf16[16,32,1024]{2,1,0:T(8,128)(2,1)S(1)} %broadcast_select_fusion), channel_id=1, replica_groups=mesh['ep'=16,'fsdp'=4,'tp'=4] {'ep'}, dimensions={0} | all-to-all | bytes 2097152 | tf_op jit(solution)/shard_map/all_to_all | solution.py:80
  58.9 0.2 reduce-scatter.3.cloned.1.call-start
  59.2 25.3 %all-gather.9.cloned.1.call-done = bf16[3145728]{0:T(1024)(128)(2,1)} async-done(((bf16[786432]{0:T(1024)(128)(2,1)}), bf16[3145728]{0:T(1024)(128)(2,1)}) %all-gather.9.cloned.1.call-update) | async-done | bytes 6291472 | tf_op jit(solution)/shard_map/all_gather | solution.py:15
  84.5 7.8 %reshape.171 = bf16[4,786432]{1,0:T(4,128)(2,1)} reshape(bf16[3145728]{0:T(1024)(128)(2,1)} %all-gather.9.cloned.1.call-done) | data formatting | bytes 12582912 | tf_op jit(solution)/shard_map/all_gather | solution.py:15
  92.3 5.4 %fusion.15 = (bf16[4,262144]{1,0:T(4,128)(2,1)}, bf16[4,262144]{1,0:T(4,128)(2,1)S(1)}, bf16[4,262144]{1,0:T(4,128)(2,1)}) fusion(bf16[4,786432]{1,0:T(4,128)(2,1)} %reshape.171), kind=kLoop, calls=%fused_computation.56 | loop fusion | bytes 12582912 | tf_op jit(solution)/shard_map/slice | solution.py:17
  97.6 3.3 squeeze_reshape_transpose_reshape.7
  100.9 3.7 %squeeze_reshape_transpose_reshape.6 = bf16[4096,256]{1,0:T(8,128)(2,1)S(1)} reshape(bf16[4,262144]{1,0:T(4,128)(2,1)} %get-tuple-element.34) | data formatting | bytes 4194304 | tf_op jit(solution)/shard_map/squeeze;reshape;transpose;reshape | solution.py:86
  104.6 3.6 %copy.64 = bf16[1,4,256,1024]{3,2,1,0:T(8,128)(2,1)} copy(bf16[1,4,256,1024]{3,1,2,0:T(4,128)(2,1)} %bitcast.71) | data formatting | bytes 4194304
  108.2 4.0 %copy.52 = bf16[1,256,4,1024]{1,3,2,0:T(8,128)(2,1)} copy(bf16[1,256,4,1024]{3,1,2,0:T(8,128)(2,1)} %bitcast.70) | data formatting | bytes 4194304 | tf_op jit(solution)/shard_map/transpose | solution.py:10
  112.1 4.3 %convolution_bitcast_fusion = f32[512,256]{0,1:T(8,128)S(1)} fusion(bf16[4096,256]{1,0:T(8,128)(2,1)} %squeeze_reshape_transpose_reshape.7, bf16[512,4096]{1,0:T(8,128)(2,1)} %bitcast.85), kind=kOutput, calls=%fused_computation.11 | convolution fusion | flops 1073741824 | bytes 6815744 | tf_op jit(solution)/shard_map/dot_general | solution.py:88
  116.5 2.1 convolution_bitcast_fusion.1
  118.6 19.2 %all-gather.5.cloned.1.call-done = bf16[512,4096]{1,0:T(8,128)(2,1)} async-done(((bf16[512,1024]{1,0:T(8,128)(2,1)}), bf16[512,4096]{1,0:T(8,128)(2,1)}) %all-gather.5.cloned.1.call-update) | async-done | bytes 4194320 | tf_op jit(solution)/shard_map/all_gather | solution.py:83
  137.8 4.5 %multiply_reduce_fusion = (bf16[512]{0:T(512)(128)(2,1)S(1)}, bf16[512,256]{0,1:T(8,128)(2,1)S(1)}, bf16[512,256]{0,1:T(8,128)(2,1)S(1)}, bf16[512,256]{0,1:T(8,128)(2,1)S(1)}) fusion(f32[512,256]{0,1:T(8,128)} %convolution_bitcast_fusion.1, f32[512,256]{0,1:T(8,128)S(1)} %convolution_bitcast_fusion, bf16[512,4096]{1,0:T(8,128)(2,1)} %all-gather.5.cloned.1.call-done, ...), kind=kOutput, calls=%fused_computation.23 | convolution fusion | flops 1076100608 | bytes 8127488 | tf_op jit(solution)/shard_map/dot_general | solution.py:63
  142.3 1.3 fusion.16
  143.7 3.4 add_convert_fusion
  147.1 0.1 all_to_all.14
  147.1 6.6 %psum.7 = bf16[16,1,32]{2,0,1:T(8,128)(2,1)S(1)} all-reduce(bf16[16,1,32]{2,0,1:T(8,128)(2,1)S(1)} %all_to_all.14), channel_id=1, replica_groups=mesh['ep'=16,'fsdp'=4,'tp'=4] {'tp'}, use_global_device_ids=true, to_apply=%region_9.10 | all-reduce | flops 512 | bytes 2048 | tf_op jit(solution)/shard_map/psum | solution.py:118
  153.7 16.9 %all_to_all.20 = bf16[16,1,32]{2,1,0:T(2,128)(2,1)S(1)} all-to-all(bf16[16,1,32]{2,1,0:T(2,128)(2,1)S(1)} %copy.53), channel_id=1, replica_groups=mesh['ep'=16,'fsdp'=4,'tp'=4] {'ep'}, dimensions={0} | all-to-all | bytes 2048 | tf_op jit(solution)/shard_map/all_to_all | solution.py:125
  170.7 26.4 %reduce-scatter.3.cloned.1.call-done = bf16[512,1024]{1,0:T(8,128)(2,1)} async-done(((bf16[512,4096]{1,0:T(8,128)(2,1)}), bf16[512,1024]{1,0:T(8,128)(2,1)}) %reduce-scatter.3.cloned.1.call-update) | async-done | bytes 1048592 | tf_op jit(solution)/shard_map/reduce_scatter | solution.py:115
  197.1 7.7 %all-to-all-start.1 = ((bf16[16,32,1024]{2,1,0:T(8,128)(2,1)}), bf16[16,32,1024]{2,1,0:T(8,128)(2,1)S(1)}, u32[]{:S(2)}, u32[]{:S(2)}) async-start(bf16[16,32,1024]{2,1,0:T(8,128)(2,1)} %bitcast.78), calls=%async_computation.2 | async-start | bytes 2097152 | tf_op jit(solution)/shard_map/all_to_all | solution.py:124
  204.9 0.1 reduce_sum.53
  205.1 0.1 reshape.138
  205.2 1.9 gather_fusion.2
  207.2 0.2 gather.23
  207.3 0.1 copy.54
  207.4 0.1 copy.49
  207.6 25.2 %all-to-all-done.1 = bf16[16,32,1024]{2,1,0:T(8,128)(2,1)S(1)} async-done(((bf16[16,32,1024]{2,1,0:T(8,128)(2,1)}), bf16[16,32,1024]{2,1,0:T(8,128)(2,1)S(1)}, u32[]{:S(2)}, u32[]{:S(2)}) %all-to-all-start.1) | async-done | bytes 1048608 | tf_op jit(solution)/shard_map/all_to_all | solution.py:124
  232.8 1.2 gather_fusion.1
  234.0 0.2 gather.21
  234.2 1.9 fusion.1
  236.1 0.3 reduce-scatter.5.cloned.1.call-start
  236.4 3.7 %convolution_convert_fusion.1 = bf16[4096,256]{0,1:T(8,128)(2,1)S(1)} fusion(bf16[512,256]{0,1:T(8,128)(2,1)S(1)} %get-tuple-element.33, bf16[512,4096]{1,0:T(8,128)(2,1)} %all-gather.5.cloned.1.call-done), kind=kOutput, calls=%fused_computation.8 | convolution fusion | flops 1074790400 | bytes 6553600 | tf_op jit(solution)/shard_map/dot_general | solution.py:57
  240.1 2.4 fusion
  242.5 3.4 %pad_maximum_fusion = bf16[4096,768]{0,1:T(8,128)(2,1)} fusion(bf16[4096,256]{0,1:T(8,128)(2,1)S(1)} %convolution_convert_fusion.1, bf16[4096,512]{0,1:T(8,128)(2,1)S(1)} %fusion), kind=kLoop, calls=%fused_computation.5 | loop fusion | flops 12582912 | bytes 12582912 | tf_op jit(solution)/shard_map/concatenate | solution.py:107
  245.9 0.6 convert_subtract_fusion
  246.5 9.8 %all-gather.7.cloned.1.call-done = bf16[128,4096]{1,0:T(8,128)(2,1)} async-done(((bf16[128,1024]{1,0:T(8,128)(2,1)}), bf16[128,4096]{1,0:T(8,128)(2,1)}) %all-gather.7.cloned.1.call-update) | async-done | bytes 1048592 | tf_op jit(solution)/shard_map/all_gather | solution.py:128
  256.3 71.3 %reduce-scatter.5.cloned.1.call-done = bf16[1024,768]{0,1:T(8,128)(2,1)} async-done(((bf16[4096,768]{0,1:T(8,128)(2,1)}), bf16[1024,768]{0,1:T(8,128)(2,1)}) %reduce-scatter.5.cloned.1.call-update) | async-done | bytes 1572880 | tf_op jit(solution)/shard_map/reduce_scatter | solution.py:25
  327.6 1.8 convert_element_type.58
  329.4 1.2 slice_bitcast_fusion
  330.6 1.3 copy.55
  331.9 1.3 copy.56
  333.2 1.0 copy.66
  (38 shorter events, 0.6 us)
Async XLA Ops:
  7.2 77.3 %all-gather.9.cloned.1.call-start = ((), (), s32[]{:S(2)}) async-start(), calls=%async_computation.9 | async-start | bytes 7864320 | tf_op jit(solution)/shard_map/all_gather | solution.py:15
  10.1 2.5 copy-start.3
  12.5 2.6 copy-start.2
  12.6 125.2 %all-gather.5.cloned.1.call-start = ((), (), s32[]{:S(2)}) async-start(), calls=%async_computation.5 | async-start | bytes 5242880 | tf_op jit(solution)/shard_map/all_gather | solution.py:83
  58.9 138.1 %reduce-scatter.3.cloned.1.call-start = ((), (), s32[]{:S(2)}) async-start(), calls=%async_computation.6 | async-start | bytes 5242880 | tf_op jit(solution)/shard_map/reduce_scatter | solution.py:115
  112.1 4.4 %copy-start.4 = (bf16[1,16,1,32,4096]{4,3,2,1,0:T(8,128)(2,1)S(1)}, bf16[1,16,1,32,4096]{4,3,2,1,0:T(8,128)(2,1)}, u32[]{:S(2)}) copy-start(bf16[1,16,1,32,4096]{4,3,2,1,0:T(8,128)(2,1)} %param.10) | copy-start | bytes 12582916
  137.8 4.5 %copy-start = (bf16[4096,256]{1,0:T(8,128)(2,1)S(1)}, bf16[4096,256]{1,0:T(8,128)(2,1)}, u32[]{:S(2)}) copy-start(bf16[4096,256]{1,0:T(8,128)(2,1)} %squeeze_reshape_transpose_reshape.7) | copy-start | bytes 6291460
  197.1 35.7 %all-to-all-start.1 = ((bf16[16,32,1024]{2,1,0:T(8,128)(2,1)}), bf16[16,32,1024]{2,1,0:T(8,128)(2,1)S(1)}, u32[]{:S(2)}, u32[]{:S(2)}) async-start(bf16[16,32,1024]{2,1,0:T(8,128)(2,1)} %bitcast.78), calls=%async_computation.2 | async-start | bytes 2097152 | tf_op jit(solution)/shard_map/all_to_all | solution.py:124
  204.8 51.5 %all-gather.7.cloned.1.call-start = ((), (), s32[]{:S(2)}) async-start(), calls=%async_computation.7 | async-start | bytes 1310720 | tf_op jit(solution)/shard_map/all_gather | solution.py:128
  236.1 91.6 %reduce-scatter.5.cloned.1.call-start = ((), (), s32[]{:S(2)}) async-start(), calls=%async_computation.8 | async-start | bytes 7864320 | tf_op jit(solution)/shard_map/reduce_scatter | solution.py:25
  236.4 3.7 %copy-start.5 = (bf16[1,16,1,32,4096]{4,3,2,1,0:T(8,128)(2,1)S(1)}, bf16[1,16,1,32,4096]{4,3,2,1,0:T(8,128)(2,1)}, u32[]{:S(2)}) copy-start(bf16[1,16,1,32,4096]{4,3,2,1,0:T(8,128)(2,1)} %param.10) | copy-start | bytes 12582916
  330.6 2.6 copy-start.1
Sparse Core Ops, SparseCore 0:
  12.7 71.7 all-gather.8
  86.3 51.4 all-gather.4
  147.2 49.8 reduce-scatter.2
  236.2 20.0 all-gather.6
  258.7 68.8 reduce-scatter.4
where the time goes:
time: 341 us
  waiting for transfers between devices  177 us (52%)
  blocking collectives  61.8 us (18%)
  local copies, waits for them, and re-layouts  46.3 us (14%)
  matrix products  21.7 us (6%)
  between operations  14.1 us (4%)
  other arithmetic  11.1 us (3%)
  starting transfers between devices  8.39 us (2%)
    reduce_scatter x1, waiting for transfers between devices, own_rows(): lax.psum_scatter(whole, axis, scatter_dimension=0, tiled=True)  71.3 us
    all_to_all x1, blocking collectives, on_device(): lax.all_to_all(outgoing.reshape(experts, capacity, narrow), 'ep', split_a...  38.3 us
    reduce_scatter x1, waiting for transfers between devices, on_device(): lax.psum_scatter(slot_part.astype(jnp.bfloat16), 'tp', scatter_dimension=...  26.4 us
    all_gather x1, waiting for transfers between devices, gather_together(): lines, at, outs = (lax.all_gather(ravelled, axis), 0, [])  25.3 us
    all_to_all x1, waiting for transfers between devices, on_device(): lax.all_to_all(leaving[0], 'ep', split_axis=0, concat_axis=0, tiled=True)  25.2 us
    all_gather x1, waiting for transfers between devices, on_device(): lax.all_gather(arrived.reshape(-1, narrow), 'tp', axis=1, tiled=True)  19.2 us
    all_to_all x1, blocking collectives, on_device(): lax.all_to_all(leaving[1], 'ep', split_axis=0, concat_axis=0, tiled=True)  16.9 us
    unnamed x20, local copies, waits for them, and re-layouts  11.3 us
  transfers between devices with their start and end apart: 6, of which 6 were waited for; matrix products, arithmetic and copies ran while one was open for 16% of the time, Pallas kernels for 0%

commit v1 on v0

--- a/solution.py
+++ b/solution.py
@@ -80,7 +80,10 @@
     arrived = lax.all_to_all(
         outgoing.reshape(experts, capacity, narrow), "ep", split_axis=0, concat_axis=0, tiled=True
     )
-    scaled = lax.all_gather(arrived.reshape(-1, narrow), "tp", axis=1, tiled=True)
+    scaled = jnp.concatenate(
+        lax.all_to_all(jnp.stack([arrived.reshape(-1, narrow)] * lax.axis_size("tp")), "tp", 0, 0),
+        axis=1,
+    )
     gate_full, up_full, down_full = gather_together((w_gate, w_up, w_down), "fsdp", (1, 1, 2))
     gate_full = gate_full[0]
     up_full = up_full[0]

time: 341 us -> 322 us (0.944)
  waiting for transfers between devices: 177 us -> 149 us
  starting transfers between devices: 8.39 us -> 13.3 us
    all_gather x1 -> x0, waiting for transfers between devices: 19.2 us -> none  [on_device(): lax.all_gather(arrived.reshape(-1, narrow), 'tp', axis=1, tiled=True)]
    all_gather x1, waiting for transfers between devices: 25.3 us -> 17.8 us  [gather_together(): lines, at, outs = (lax.all_gather(ravelled, axis), 0, [])]
    all_to_all x0 -> x1, starting transfers between devices: none -> 4.94 us  [on_device(): lax.all_to_all(jnp.stack([arrived.reshape(-1, narrow)] * lax.axis_size('t...]
  transfers between devices with their start and end apart: 6 -> 6, of which waited for: 6 -> 5; matrix products, arithmetic and copies ran while one was open for 16% -> 18% of each run, Pallas kernels for 0% -> 0%
where the time goes in v1:
time: 322 us
  waiting for transfers between devices  149 us (46%)
  blocking collectives  63.4 us (20%)
  local copies, waits for them, and re-layouts  48.9 us (15%)
  matrix products  21.7 us (7%)
  between operations  14.1 us (4%)
  starting transfers between devices  13.3 us (4%)
  other arithmetic  11.1 us (3%)
    reduce_scatter x1, waiting for transfers between devices, own_rows(): lax.psum_scatter(whole, axis, scatter_dimension=0, tiled=True)  71.3 us
    all_to_all x1, blocking collectives, on_device(): lax.all_to_all(outgoing.reshape(experts, capacity, narrow), 'ep', split_a...  38.2 us
    all_to_all x1, waiting for transfers between devices, on_device(): lax.all_to_all(leaving[0], 'ep', split_axis=0, concat_axis=0, tiled=True)  25.2 us
    reduce_scatter x1, waiting for transfers between devices, on_device(): lax.psum_scatter(slot_part.astype(jnp.bfloat16), 'tp', scatter_dimension=...  25.1 us
    all_gather x1, waiting for transfers between devices, gather_together(): lines, at, outs = (lax.all_gather(ravelled, axis), 0, [])  17.8 us
    all_to_all x1, blocking collectives, on_device(): lax.all_to_all(leaving[1], 'ep', split_axis=0, concat_axis=0, tiled=True)  16.7 us
    unnamed x20, local copies, waits for them, and re-layouts  11.3 us
    all_gather x1, waiting for transfers between devices, on_device(): input_grad = lax.all_gather(combined, 'tp', axis=1, tiled=True)  9.73 us
  transfers between devices with their start and end apart: 6, of which 5 were waited for; matrix products, arithmetic and copies ran while one was open for 18% of the time, Pallas kernels for 0%

profile of v1, /device:TPU:1, one launch (start us, length us, event | category | flops | bytes accessed | tf_op | source)
XLA Modules:
  0.0 321.6 jit_solution(8286597631055667036)
XLA Ops:
  7.2 1.5 copy.62
  8.7 1.5 copy.63
  10.1 1.1 copy.64
  11.3 1.2 pad_maximum_fusion.1
  12.6 0.1 copy.48
  12.7 0.1 eq.26
  12.8 0.1 reshape.133
  13.0 1.0 dynamic-slice_convert_fusion
  14.0 0.4 mul.83
  14.3 0.7 mul.84
  15.1 0.1 copy.54
  15.3 0.1 mul.80
  15.4 0.6 reduce-window.6
  16.0 0.2 slice_reduce_fusion
  16.2 0.1 copy.53
  16.4 0.1 mul.79
  16.5 0.1 fusion.8
  16.6 1.4 scatter_custom_fusion
  18.0 0.1 broadcast_in_dim.52
  18.1 0.1 multiply_convert_fusion
  18.3 2.1 gather_fusion
  20.4 0.2 broadcast_select_fusion
  20.5 38.2 %all_to_all.24 = bf16[16,32,1024]{2,1,0:T(8,128)(2,1)S(1)} all-to-all(bf16[16,32,1024]{2,1,0:T(8,128)(2,1)S(1)} %broadcast_select_fusion), channel_id=1, replica_groups=mesh['ep'=16,'fsdp'=4,'tp'=4] {'ep'}, dimensions={0} | all-to-all | bytes 2097152 | tf_op jit(solution)/shard_map/all_to_all | solution.py:80
  58.8 0.5 copy.55
  59.3 2.3 stack.3
  61.6 4.9 %all-to-all-start.1 = ((bf16[4,512,1024]{1,2,0:T(8,128)(2,1)}), bf16[4,512,1024]{1,2,0:T(8,128)(2,1)}, u32[]{:S(2)}, u32[]{:S(2)}) async-start(bf16[4,512,1024]{1,2,0:T(8,128)(2,1)} %stack.3), calls=%async_computation.1 | async-start | bytes 8388608 | tf_op jit(solution)/shard_map/all_to_all | solution.py:84
  66.5 0.2 reduce-scatter.3.cloned.1.call-start
  66.7 17.8 %all-gather.6.cloned.1.call-done = bf16[3145728]{0:T(1024)(128)(2,1)} async-done(((bf16[786432]{0:T(1024)(128)(2,1)}), bf16[3145728]{0:T(1024)(128)(2,1)}) %all-gather.6.cloned.1.call-update) | async-done | bytes 6291472 | tf_op jit(solution)/shard_map/all_gather | solution.py:15
  84.5 7.8 %reshape.177 = bf16[4,786432]{1,0:T(4,128)(2,1)} reshape(bf16[3145728]{0:T(1024)(128)(2,1)} %all-gather.6.cloned.1.call-done) | data formatting | bytes 12582912 | tf_op jit(solution)/shard_map/all_gather | solution.py:15
  92.3 5.4 %fusion.15 = (bf16[4,262144]{1,0:T(4,128)(2,1)}, bf16[4,262144]{1,0:T(4,128)(2,1)S(1)}, bf16[4,262144]{1,0:T(4,128)(2,1)}) fusion(bf16[4,786432]{1,0:T(4,128)(2,1)} %reshape.177), kind=kLoop, calls=%fused_computation.56 | loop fusion | bytes 12582912 | tf_op jit(solution)/shard_map/slice | solution.py:17
  97.6 3.3 %squeeze_reshape_transpose_reshape.7 = bf16[4096,256]{1,0:T(8,128)(2,1)} reshape(bf16[4,262144]{1,0:T(4,128)(2,1)S(1)} %get-tuple-element.35) | data formatting | bytes 4194304 | tf_op jit(solution)/shard_map/squeeze;reshape;transpose;reshape | solution.py:88
  100.9 3.5 %squeeze_reshape_transpose_reshape.6 = bf16[4096,256]{1,0:T(8,128)(2,1)S(1)} reshape(bf16[4,262144]{1,0:T(4,128)(2,1)} %get-tuple-element.34) | data formatting | bytes 4194304 | tf_op jit(solution)/shard_map/squeeze;reshape;transpose;reshape | solution.py:89
  104.4 3.6 %copy.68 = bf16[1,4,256,1024]{3,2,1,0:T(8,128)(2,1)} copy(bf16[1,4,256,1024]{3,1,2,0:T(4,128)(2,1)} %bitcast.74) | data formatting | bytes 4194304
  108.0 3.9 %copy.56 = bf16[1,256,4,1024]{1,3,2,0:T(8,128)(2,1)} copy(bf16[1,256,4,1024]{3,1,2,0:T(8,128)(2,1)} %bitcast.73) | data formatting | bytes 4194304 | tf_op jit(solution)/shard_map/transpose | solution.py:10
  111.9 4.3 %convolution_bitcast_fusion = f32[512,256]{0,1:T(8,128)S(1)} fusion(bf16[4096,256]{1,0:T(8,128)(2,1)} %squeeze_reshape_transpose_reshape.7, bf16[512,4096]{1,0:T(8,128)(2,1)} %bitcast.88), kind=kOutput, calls=%fused_computation.11 | convolution fusion | flops 1073741824 | bytes 6815744 | tf_op jit(solution)/shard_map/dot_general | solution.py:91
  116.2 2.1 convolution_bitcast_fusion.1
  118.3 4.5 %multiply_reduce_fusion = (bf16[512]{0:T(512)(128)(2,1)S(1)}, bf16[512,256]{0,1:T(8,128)(2,1)S(1)}, bf16[512,256]{0,1:T(8,128)(2,1)S(1)}, bf16[512,256]{0,1:T(8,128)(2,1)S(1)}) fusion(f32[512,256]{0,1:T(8,128)} %convolution_bitcast_fusion.1, f32[512,256]{0,1:T(8,128)S(1)} %convolution_bitcast_fusion, bf16[512,4096]{0,1:T(8,128)(2,1)} %bitcast.6, ...), kind=kOutput, calls=%fused_computation.23 | convolution fusion | flops 1076100608 | bytes 8127488 | tf_op jit(solution)/shard_map/dot_general | solution.py:63
  122.9 1.3 fusion.16
  124.2 3.4 %add_convert_fusion = bf16[512,4096]{1,0:T(8,128)(2,1)} fusion(f32[512,4096]{1,0:T(8,128)S(1)} %fusion.16, bf16[512,256]{0,1:T(8,128)(2,1)S(1)} %get-tuple-element.41, bf16[4096,256]{1,0:T(8,128)(2,1)S(1)} %squeeze_reshape_transpose_reshape.6), kind=kOutput, calls=%fused_computation.4 | convolution fusion | flops 1077936128 | bytes 14942208 | tf_op jit(solution)/shard_map/dot_general | solution.py:63
  127.6 8.4 %psum.7 = bf16[16,1,32]{2,0,1:T(8,128)(2,1)S(1)} all-reduce(bf16[16,1,32]{2,0,1:T(8,128)(2,1)S(1)} %all_to_all.18), channel_id=1, replica_groups=mesh['ep'=16,'fsdp'=4,'tp'=4] {'tp'}, use_global_device_ids=true, to_apply=%region_9.10 | all-reduce | flops 512 | bytes 2048 | tf_op jit(solution)/shard_map/psum | solution.py:121
  136.1 16.7 %all_to_all.25 = bf16[16,1,32]{2,1,0:T(2,128)(2,1)S(1)} all-to-all(bf16[16,1,32]{2,1,0:T(2,128)(2,1)S(1)} %copy.57), channel_id=1, replica_groups=mesh['ep'=16,'fsdp'=4,'tp'=4] {'ep'}, dimensions={0} | all-to-all | bytes 2048 | tf_op jit(solution)/shard_map/all_to_all | solution.py:128
  152.8 25.1 %reduce-scatter.3.cloned.1.call-done = bf16[512,1024]{1,0:T(8,128)(2,1)} async-done(((bf16[512,4096]{1,0:T(8,128)(2,1)}), bf16[512,1024]{1,0:T(8,128)(2,1)}) %reduce-scatter.3.cloned.1.call-update) | async-done | bytes 1048592 | tf_op jit(solution)/shard_map/reduce_scatter | solution.py:118
  177.9 7.8 %all-to-all-start.2 = ((bf16[16,32,1024]{2,1,0:T(8,128)(2,1)}), bf16[16,32,1024]{2,1,0:T(8,128)(2,1)S(1)}, u32[]{:S(2)}, u32[]{:S(2)}) async-start(bf16[16,32,1024]{2,1,0:T(8,128)(2,1)} %bitcast.81), calls=%async_computation.3 | async-start | bytes 2097152 | tf_op jit(solution)/shard_map/all_to_all | solution.py:127
  185.7 0.1 reduce_sum.53
  186.0 0.1 reshape.144
  186.1 1.9 gather_fusion.2
  188.0 0.2 gather.23
  188.3 0.1 copy.52
  188.4 25.2 %all-to-all-done.2 = bf16[16,32,1024]{2,1,0:T(8,128)(2,1)S(1)} async-done(((bf16[16,32,1024]{2,1,0:T(8,128)(2,1)}), bf16[16,32,1024]{2,1,0:T(8,128)(2,1)S(1)}, u32[]{:S(2)}, u32[]{:S(2)}) %all-to-all-start.2) | async-done | bytes 1048608 | tf_op jit(solution)/shard_map/all_to_all | solution.py:127
  213.7 1.2 gather_fusion.1
  214.8 0.2 gather.21
  215.1 1.9 fusion.1
  216.9 0.3 reduce-scatter.5.cloned.1.call-start
  217.3 3.7 %convolution_convert_fusion.1 = bf16[4096,256]{0,1:T(8,128)(2,1)S(1)} fusion(bf16[512,4096]{0,1:T(8,128)(2,1)} %bitcast.6, bf16[512,256]{0,1:T(8,128)(2,1)S(1)} %get-tuple-element.33), kind=kOutput, calls=%fused_computation.8 | convolution fusion | flops 1074790400 | bytes 6553600 | tf_op jit(solution)/shard_map/dot_general | solution.py:57
  221.0 2.4 fusion
  223.4 3.4 %pad_maximum_fusion = bf16[4096,768]{0,1:T(8,128)(2,1)} fusion(bf16[4096,256]{0,1:T(8,128)(2,1)S(1)} %convolution_convert_fusion.1, bf16[4096,512]{0,1:T(8,128)(2,1)S(1)} %fusion), kind=kLoop, calls=%fused_computation.5 | loop fusion | flops 12582912 | bytes 12582912 | tf_op jit(solution)/shard_map/concatenate | solution.py:110
  226.9 0.6 convert_subtract_fusion
  227.4 9.7 %all-gather.4.cloned.1.call-done = bf16[128,4096]{1,0:T(8,128)(2,1)} async-done(((bf16[128,1024]{1,0:T(8,128)(2,1)}), bf16[128,4096]{1,0:T(8,128)(2,1)}) %all-gather.4.cloned.1.call-update) | async-done | bytes 1048592 | tf_op jit(solution)/shard_map/all_gather | solution.py:131
  237.2 71.3 %reduce-scatter.5.cloned.1.call-done = bf16[1024,768]{0,1:T(8,128)(2,1)} async-done(((bf16[4096,768]{0,1:T(8,128)(2,1)}), bf16[1024,768]{0,1:T(8,128)(2,1)}) %reduce-scatter.5.cloned.1.call-update) | async-done | bytes 1572880 | tf_op jit(solution)/shard_map/reduce_scatter | solution.py:25
  308.5 1.8 convert_element_type.58
  310.3 1.2 slice_bitcast_fusion
  311.5 1.3 copy.59
  312.8 1.3 copy.60
  314.1 1.0 copy.70
  (39 shorter events, 0.7 us)
Async XLA Ops:
  7.2 77.3 %all-gather.6.cloned.1.call-start = ((), (), s32[]{:S(2)}) async-start(), calls=%async_computation.9 | async-start | bytes 7864320 | tf_op jit(solution)/shard_map/all_gather | solution.py:15
  10.1 2.4 copy-start.3
  12.5 2.5 copy-start.2
  61.6 56.8 %all-to-all-start.1 = ((bf16[4,512,1024]{1,2,0:T(8,128)(2,1)}), bf16[4,512,1024]{1,2,0:T(8,128)(2,1)}, u32[]{:S(2)}, u32[]{:S(2)}) async-start(bf16[4,512,1024]{1,2,0:T(8,128)(2,1)} %stack.3), calls=%async_computation.1 | async-start | bytes 8388608 | tf_op jit(solution)/shard_map/all_to_all | solution.py:84
  66.5 111.4 %reduce-scatter.3.cloned.1.call-start = ((), (), s32[]{:S(2)}) async-start(), calls=%async_computation.6 | async-start | bytes 5242880 | tf_op jit(solution)/shard_map/reduce_scatter | solution.py:118
  111.9 4.3 %copy-start.4 = (bf16[1,16,1,32,4096]{4,3,2,1,0:T(8,128)(2,1)S(1)}, bf16[1,16,1,32,4096]{4,3,2,1,0:T(8,128)(2,1)}, u32[]{:S(2)}) copy-start(bf16[1,16,1,32,4096]{4,3,2,1,0:T(8,128)(2,1)} %param.10) | copy-start | bytes 12582916
  118.3 4.5 %copy-start = (bf16[4096,256]{1,0:T(8,128)(2,1)S(1)}, bf16[4096,256]{1,0:T(8,128)(2,1)}, u32[]{:S(2)}) copy-start(bf16[4096,256]{1,0:T(8,128)(2,1)} %squeeze_reshape_transpose_reshape.7) | copy-start | bytes 6291460
  177.9 35.8 %all-to-all-start.2 = ((bf16[16,32,1024]{2,1,0:T(8,128)(2,1)}), bf16[16,32,1024]{2,1,0:T(8,128)(2,1)S(1)}, u32[]{:S(2)}, u32[]{:S(2)}) async-start(bf16[16,32,1024]{2,1,0:T(8,128)(2,1)} %bitcast.81), calls=%async_computation.3 | async-start | bytes 2097152 | tf_op jit(solution)/shard_map/all_to_all | solution.py:127
  185.7 51.5 %all-gather.4.cloned.1.call-start = ((), (), s32[]{:S(2)}) async-start(), calls=%async_computation.7 | async-start | bytes 1310720 | tf_op jit(solution)/shard_map/all_gather | solution.py:131
  216.9 91.6 %reduce-scatter.5.cloned.1.call-start = ((), (), s32[]{:S(2)}) async-start(), calls=%async_computation.8 | async-start | bytes 7864320 | tf_op jit(solution)/shard_map/reduce_scatter | solution.py:25
  217.2 3.7 %copy-start.5 = (bf16[1,16,1,32,4096]{4,3,2,1,0:T(8,128)(2,1)S(1)}, bf16[1,16,1,32,4096]{4,3,2,1,0:T(8,128)(2,1)}, u32[]{:S(2)}) copy-start(bf16[1,16,1,32,4096]{4,3,2,1,0:T(8,128)(2,1)} %param.10) | copy-start | bytes 12582916
  311.5 2.6 copy-start.1
Sparse Core Ops, SparseCore 0:
  12.7 71.7 all-gather.5
  127.7 50.1 reduce-scatter.2
  217.1 20.0 all-gather.3
  239.6 68.8 reduce-scatter.4
